TPU v7x, 64 devices: a 2x2x8 block of a 4x4x8 slice. The times are simulated.
64 devices in a mesh: data: 4 (over x, y), seq: 16 (over z, core).
Axes of the slice: x: 2, y: 2, z: 8, core: 2. Of those that a mesh axis runs over, the one named last changes fastest.
The devices are a block of a 4x4x8 slice.
Arguments:
- x: bfloat16 [32768, 4096], P(('data', 'seq')), parts along dimension 0
- g: float32 [4096], replicated
- wqkv: bfloat16 [4096, 3, 16, 256], replicated
- wo: bfloat16 [16, 256, 4096], replicated
Outputs:
- output: bfloat16 [32768, 4096], P(('data', 'seq')), parts along dimension 0
There are 4 independent parts. A program takes and returns all parts, laid end to end along the dimension named above; an argument that names none is the same for every part.
All inputs are finite; a program needn't handle non-finite values.
Results may differ from a plain program's by a relative error of at most 0.00311508.
Values are sent between devices in bfloat16 or wider.
A program may use at most 768 MiB of HBM per device.

v0:
```python
import jax
import jax.numpy as jnp
from jax import lax
from jax.sharding import PartitionSpec as P


def _angles(pos, dh):
    half = dh // 2
    inv = 10000.0 ** (-jnp.arange(half, dtype=jnp.float32) * 2.0 / dh)
    ang = pos[:, None] * inv[None, :]
    return jnp.cos(ang)[:, None, :], jnp.sin(ang)[:, None, :]


def _rope(x, cos, sin):
    half = x.shape[-1] // 2
    x1, x2 = x[..., :half], x[..., half:]
    return jnp.concatenate([x1 * cos - x2 * sin, x2 * cos + x1 * sin], axis=-1)


def solution(mesh):
    p = mesh.shape["seq"]
    rows = P(("data", "seq"), None)

    def local(x, g, wqkv, wo):
        t, d = x.shape
        _, _, h, dh = wqkv.shape
        me = lax.axis_index("seq")
        xf = x.astype(jnp.float32)
        xn = (xf * lax.rsqrt(jnp.mean(xf * xf, axis=-1, keepdims=True) + 1e-5) * g).astype(jnp.bfloat16)
        qkv = jnp.einsum("td,dchk->cthk", xn, wqkv, preferred_element_type=jnp.float32)
        pos = (me * t + jnp.arange(t)).astype(jnp.float32)
        cos, sin = _angles(pos, dh)
        buf = jnp.concatenate([_rope(qkv[:2], cos, sin), qkv[2:]], axis=0).astype(jnp.bfloat16)
        buf = lax.all_to_all(buf, "seq", 2, 1, tiled=True)
        qkv_h = buf.transpose(0, 2, 1, 3)
        q, k, v = qkv_h[0], qkv_h[1], qkv_h[2]
        scale = dh ** -0.5
        outs = []
        for j in range(p):
            lo, hi = j * t, (j + 1) * t
            sc = jnp.einsum("hqd,hkd->hqk", q[:, lo:hi], k[:, :hi], preferred_element_type=jnp.float32) * scale
            mask = (lo + jnp.arange(t))[:, None] >= jnp.arange(hi)[None, :]
            sc = jnp.where(mask, sc, -jnp.inf)
            pr = jax.nn.softmax(sc, axis=-1).astype(jnp.bfloat16)
            outs.append(jnp.einsum("hqk,hkd->hqd", pr, v[:, :hi], preferred_element_type=jnp.float32).astype(jnp.bfloat16))
        o = jnp.concatenate(outs, axis=1).transpose(1, 0, 2)
        o = lax.all_to_all(o, "seq", 0, 1, tiled=True)
        y = xf + jnp.einsum("thk,hkd->td", o, wo, preferred_element_type=jnp.float32)
        return y.astype(jnp.bfloat16)

    return jax.shard_map(local, mesh=mesh,
                         in_specs=(rows, P(None), P(None, None, None, None), P(None, None, None)),
                         out_specs=rows, check_vma=False)
```

profile of v0, /device:TPU:21, one launch (start us, length us, event | category | flops | bytes accessed | tf_op | source)
XLA Modules:
  0.0 793.1 jit_solution(7199381971211541818)
XLA Ops:
  0.0 3.1 fusion.12
  3.1 62.1 %fusion.8 = f32[3,512,16,256]{1,3,2,0:T(8,128)} fusion(bf16[4096,3,16,256]{3,2,1,0:T(8,128)(2,1)} %param.6, bf16[512,4096]{1,0:T(8,128)(2,1)} %param.4, f32[4096]{0:T(1024)S(1)} %copy-done.22, f32[512]{0:T(512)S(1)} %add_rsqrt_fusion), kind=kOutput, calls=%fused_computation.40 | convolution fusion | flops 51547996160 | bytes 130041856 | tf_op jit(solution)/shard_map/td,dchk->cthk/dot_general | solution.py:30
  65.3 4.0 slice.430
  70.2 7.3 subtract_convert_fusion
  77.6 6.3 pad_maximum_fusion
  83.9 5.5 copy.17
  89.4 22.3 %all-to-all-start = ((bf16[3,512,16,256]{1,3,0,2:T(8,128)(2,1)}), bf16[3,512,16,256]{1,3,0,2:T(8,128)(2,1)}, u32[]{:S(2)}, u32[]{:S(2)}) async-start(bf16[3,512,16,256]{1,3,0,2:T(8,128)(2,1)} %copy.17), calls=%async_computation | async-start | bytes 25165824 | tf_op jit(solution)/shard_map/all_to_all | solution.py:34
  114.2 281.8 %all-to-all-done = bf16[3,512,16,256]{1,3,0,2:T(8,128)(2,1)} async-done(((bf16[3,512,16,256]{1,3,0,2:T(8,128)(2,1)}), bf16[3,512,16,256]{1,3,0,2:T(8,128)(2,1)}, u32[]{:S(2)}, u32[]{:S(2)}) %all-to-all-start) | async-done | bytes 12582944 | tf_op jit(solution)/shard_map/all_to_all | solution.py:34
  396.0 16.5 %copy.18 = bf16[3,512,16,256]{3,1,2,0:T(8,128)(2,1)} copy(bf16[3,512,16,256]{1,3,0,2:T(8,128)(2,1)} %all-to-all-done) | data formatting | bytes 25165824 | tf_op jit(solution)/shard_map/all_to_all | solution.py:34
  412.5 6.8 fusion.94
  421.0 3.0 fusion.96
  426.3 2.9 fusion.98
  429.2 3.4 fusion.99
  433.9 4.5 fusion.101
  438.4 5.4 fusion.102
  443.7 2.5 fusion.103
  446.2 4.9 fusion.104
  451.1 4.9 fusion.105
  456.0 6.8 fusion.106
  462.8 8.2 %fusion.107 = (f32[512]{0:T(512)}, f32[512,6656]{1,0:T(8,128)}) fusion(bf16[1,8192,256]{2,1,0:T(8,128)(2,1)S(1)} %bitcast.398, bf16[1,8192,256]{2,1,0:T(8,128)(2,1)} %bitcast.412, s32[512]{0:T(512)S(1)} %copy-done.15), kind=kOutput, calls=%fused_computation.243 | convolution fusion | flops 1758461440 | bytes 17305600 | tf_op jit(solution)/shard_map/hqd,hkd->hqk/dot_general | solution.py:41
  471.0 10.6 %fusion.108 = (f32[512]{0:T(512)}, f32[512,7168]{1,0:T(8,128)}) fusion(bf16[1,8192,256]{2,1,0:T(8,128)(2,1)} %bitcast.395, bf16[1,8192,256]{2,1,0:T(8,128)(2,1)} %bitcast.413, s32[512]{0:T(512)S(1)} %iota_add_fusion.2), kind=kOutput, calls=%fused_computation.244 | convolution fusion | flops 1893727744 | bytes 18616320 | tf_op jit(solution)/shard_map/hqd,hkd->hqk/dot_general | solution.py:41
  481.5 11.1 %fusion.109 = (f32[512]{0:T(512)}, f32[512,7680]{1,0:T(8,128)}) fusion(bf16[1,8192,256]{2,1,0:T(8,128)(2,1)} %bitcast.396, bf16[1,8192,256]{2,1,0:T(8,128)(2,1)} %bitcast.414, s32[512]{0:T(512)S(1)} %iota_add_fusion.1), kind=kOutput, calls=%fused_computation.245 | convolution fusion | flops 2028994048 | bytes 19927040 | tf_op jit(solution)/shard_map/hqd,hkd->hqk/dot_general | solution.py:41
  497.0 2.4 fusion.85
  500.1 2.7 fusion.87
  503.4 3.1 fusion.63
  513.5 4.3 fusion.22
  517.8 5.7 fusion.81
  524.8 3.9 fusion.79
  530.9 2.5 fusion.59
  533.4 5.6 fusion.11
  539.0 6.8 fusion.77
  547.6 2.7 fusion.75
  550.3 6.5 fusion.6
  556.9 8.4 %fusion.73 = bf16[1,8192,256]{2,1,0:T(8,128)(2,1)} fusion(bf16[1,8192,256]{2,1,0:T(8,128)(2,1)} %fusion.75, bf16[1,8192,256]{2,1,0:T(8,128)(2,1)} %bitcast.374, f32[512,6144]{1,0:T(8,128)} %get-tuple-element.35, f32[512]{0:T(512)S(1)} %fusion.6, f32[512]{0:T(512)S(1)} %get-tuple-element.34), kind=kOutput, calls=%fused_computation.162 | convolution fusion | flops 1620180992 | bytes 15994880 | tf_op jit(solution)/shard_map/hqk,hkd->hqd/dot_general | solution.py:45
  567.3 5.3 fusion.71
  572.6 7.4 fusion.4
  580.0 7.2 fusion.69
  587.2 7.7 fusion.3
  594.9 7.8 fusion.67
  602.7 8.4 %fusion.110 = (f32[512]{0:T(512)S(1)}, f32[512,8192]{1,0:T(8,128)}) fusion(bf16[8192,256]{1,0:T(8,128)(2,1)S(1)} %bitcast.399, bf16[1,8192,256]{2,1,0:T(8,128)(2,1)} %bitcast.415, s32[512]{0:T(512)S(1)} %copy-done.14), kind=kOutput, calls=%fused_computation.246 | convolution fusion | flops 2164260352 | bytes 21237760 | tf_op jit(solution)/shard_map/hqd,hkd->hqk/dot_general | solution.py:41
  611.1 8.1 %fusion.2 = f32[512]{0:T(512)S(1)} fusion(f32[512,8192]{1,0:T(8,128)} %get-tuple-element.43, f32[512]{0:T(512)S(1)} %get-tuple-element.42), kind=kLoop, calls=%fused_computation.10 | loop fusion | flops 8388096 | bytes 16781312 | tf_op jit(solution)/shard_map/reduce_sum | solution.py:44
  619.2 9.2 %fusion.65 = bf16[1,8192,256]{2,1,0:T(8,128)(2,1)} fusion(bf16[1,8192,256]{2,1,0:T(8,128)(2,1)} %fusion.67, bf16[8192,256]{1,0:T(8,128)(2,1)S(1)} %bitcast.383, f32[512,8192]{1,0:T(8,128)} %get-tuple-element.43, f32[512]{0:T(512)S(1)} %fusion.2, f32[512]{0:T(512)S(1)} %get-tuple-element.42), kind=kOutput, calls=%fused_computation.154 | convolution fusion | flops 2160197632 | bytes 21237760 | tf_op jit(solution)/shard_map/hqk,hkd->hqd/dot_general | solution.py:45
  629.1 6.8 reduce.64
  635.9 10.5 %reshape.672 = bf16[16,2,65536]{2,1,0:T(2,128)(2,1)} reshape(bf16[8192,256]{1,0:T(8,128)(2,1)} %reduce.64) | data formatting | bytes 8388608
  646.3 101.6 %all_to_all.33 = bf16[16,2,65536]{2,1,0:T(2,128)(2,1)} all-to-all(bf16[16,2,65536]{2,1,0:T(2,128)(2,1)} %reshape.672), channel_id=1, replica_groups=mesh['data'=4,'seq'=16] {'seq'}, dimensions={0} | all-to-all | bytes 8388608 | tf_op jit(solution)/shard_map/all_to_all | solution.py:47
  747.9 12.3 %reshape.673 = bf16[8192,1,256]{2,1,0:T(2,128)(2,1)} reshape(bf16[16,2,65536]{2,1,0:T(2,128)(2,1)} %all_to_all.33) | data formatting | bytes 8388608
  760.2 6.1 copy.21
  766.3 26.5 %fusion.15 = bf16[512,4096]{1,0:T(8,128)(2,1)} fusion(bf16[512,4096]{1,0:T(8,128)(2,1)} %param.4, bf16[512,16,256]{2,0,1:T(8,128)(2,1)} %bitcast.367, bf16[16,256,4096]{2,1,0:T(8,128)(2,1)} %param.7), kind=kOutput, calls=%fused_computation.49 | convolution fusion | flops 17186160640 | bytes 46137344 | tf_op jit(solution)/shard_map/thk,hkd->td/dot_general | solution.py:48
  (101 shorter events, 29.1 us)
Async XLA Ops:
  0.0 3.1 copy-start.22
  89.4 306.6 %all-to-all-start = ((bf16[3,512,16,256]{1,3,0,2:T(8,128)(2,1)}), bf16[3,512,16,256]{1,3,0,2:T(8,128)(2,1)}, u32[]{:S(2)}, u32[]{:S(2)}) async-start(bf16[3,512,16,256]{1,3,0,2:T(8,128)(2,1)} %copy.17), calls=%async_computation | async-start | bytes 25165824 | tf_op jit(solution)/shard_map/all_to_all | solution.py:34
  419.4 26.8 %copy-start.5 = (bf16[1,16,512,1,256]{4,2,1,3,0:T(8,128)(2,1)}, bf16[1,16,512,1,256]{4,2,1,3,0:T(8,128)(2,1)S(1)}, u32[]{:S(2)}) copy-start(bf16[1,16,512,1,256]{4,2,1,3,0:T(8,128)(2,1)S(1)} %get-tuple-element.8) | copy-start | bytes 12582916
  419.4 26.8 %copy-start.8 = (bf16[1,16,512,1,256]{4,2,1,3,0:T(8,128)(2,1)}, bf16[1,16,512,1,256]{4,2,1,3,0:T(8,128)(2,1)S(1)}, u32[]{:S(2)}) copy-start(bf16[1,16,512,1,256]{4,2,1,3,0:T(8,128)(2,1)S(1)} %get-tuple-element.9) | copy-start | bytes 12582916
  443.7 2.5 copy-start.17
  451.1 4.9 copy-start.6
  451.1 4.9 copy-start.16
  456.0 6.8 copy-start.15
  492.6 3.9 copy-start.10
  492.6 3.9 copy-start.18
  497.0 2.4 copy-start.9
  500.0 2.7 copy-start
  502.7 3.9 slice-start.6
  503.4 3.2 slice-start.7
  506.6 2.2 copy-start.1
  513.5 10.1 %slice-start.4 = ((s8[8388608]{0:T(1024)(128)(4,1)}), s8[4194304]{0:T(1024)(128)(4,1)S(1)}, s32[]{:S(2)}) async-start(s8[8388608]{0:T(1024)(128)(4,1)} %bitcast.363), calls=%async_computation.6 | async-start | bytes 8388608
  517.8 5.8 slice-start.5
  517.8 5.7 copy-start.21
  524.8 3.9 copy-start.20
  528.7 2.2 copy-start.2
  533.4 5.7 copy-start.3
  539.0 6.8 copy-start.19
  550.3 14.9 %slice-start = ((s8[13631488]{0:T(1024)(128)(4,1)}), s8[4194304]{0:T(1024)(128)(4,1)S(1)}, s32[]{:S(2)}) async-start(s8[13631488]{0:T(1024)(128)(4,1)} %bitcast.361), calls=%async_computation.2 | async-start | bytes 8388608
  556.8 8.4 %slice-start.1 = ((s8[13631488]{0:T(1024)(128)(4,1)}), s8[4194304]{0:T(1024)(128)(4,1)S(1)}, s32[]{:S(2)}) async-start(s8[13631488]{0:T(1024)(128)(4,1)} %bitcast.361), calls=%async_computation.3 | async-start | bytes 8388608
  556.8 8.4 %slice-start.2 = ((s8[13631488]{0:T(1024)(128)(4,1)}), s8[4194304]{0:T(1024)(128)(4,1)S(1)}, s32[]{:S(2)}) async-start(s8[13631488]{0:T(1024)(128)(4,1)} %bitcast.361), calls=%async_computation.4 | async-start | bytes 8388608
  556.9 8.4 %slice-start.3 = ((s8[13631488]{0:T(1024)(128)(4,1)}), s8[1048576]{0:T(1024)(128)(4,1)S(1)}, s32[]{:S(2)}) async-start(s8[13631488]{0:T(1024)(128)(4,1)} %bitcast.361), calls=%async_computation.5 | async-start | bytes 2097152
  556.9 8.4 %copy-start.13 = (f32[512]{0:T(512)S(1)}, f32[512]{0:T(512)}, u32[]{:S(2)}) copy-start(f32[512]{0:T(512)} %get-tuple-element.36) | copy-start | bytes 6148
  567.3 5.3 copy-start.12
  572.6 7.4 copy-start.4
  580.0 7.2 copy-start.11
  594.9 7.8 copy-start.7
  594.9 7.8 copy-start.14
where the time goes:
time: 797 us; the launch traced here: 793 us
  waiting for transfers between devices  282 us (35%)
  matrix products  244 us (31%)
  blocking collectives  102 us (13%)
  other arithmetic  78.3 us (10%)
  local copies, waits for them, and re-layouts  64.5 us (8%)
  starting transfers between devices  22.3 us (3%)
    all_to_all x1, waiting for transfers between devices, local(): buf = lax.all_to_all(buf, 'seq', 2, 1, tiled=True)  282 us
    all_to_all x1, blocking collectives, local(): o = lax.all_to_all(o, 'seq', 0, 1, tiled=True)  102 us
    dot_general x16, matrix products, local(): jnp.einsum('hqd,hkd->hqk', q[:, lo:hi], k[:, :hi], preferred_element_type...  81.6 us
    dot_general x16, matrix products, local(): jnp.einsum('hqk,hkd->hqd', pr, v[:, :hi], preferred_element_type=jnp.floa...  73.7 us
    dot_general x1, matrix products, local(): jnp.einsum('td,dchk->cthk', xn, wqkv, preferred_element_type=jnp.float32)  62.1 us
    reduce_sum x16, other arithmetic, local(): pr = jax.nn.softmax(sc, axis=-1).astype(jnp.bfloat16)  51.4 us
    unnamed x65, local copies, waits for them, and re-layouts  31.1 us
    dot_general x1, matrix products, local(): jnp.einsum('thk,hkd->td', o, wo, preferred_element_type=jnp.float32)  26.5 us
  transfers between devices with their start and end apart: 1, of which 1 were waited for; matrix products, arithmetic and copies ran while one was open for 0% of the time, Pallas kernels for 0%

commit v1 on v0

v1 whole, which is shorter than its diff:
```python
import functools

import jax
import jax.numpy as jnp
import numpy as np
from jax import lax
from jax.experimental import pallas as pl
from jax.experimental.pallas import tpu as pltpu
from jax.sharding import PartitionSpec as P

BF = jnp.bfloat16
F32 = jnp.float32
I32 = jnp.int32
VMEM_LIMIT = 63 * 2**20
R = 256

OWN, N1A, N1B, FWA, N2A, FWB, N2B = range(7)


def _pick(i, values):
    out = jnp.asarray(values[0], I32)
    for n, v in enumerate(values[1:], 1):
        out = jnp.where(i == n, v, out)
    return out


def _mega_body(p, x_ref, g_ref, w_ref, cosb, sinb, cosc, sinc, o_ref, wall, xb,
               kvs, qs, xv, wt, sa, sb, acc, ms, ls, fb, ob, cs, sn, pin, pout,
               ld_sem, wt_sem, pi_sem, po_sem, xs_sem, xr_sem, fs_sem, fr_sem, os_sem, or_sem):
    nchip = p // 2
    ng = nchip // 2
    d = x_ref.shape[1]
    t_rows = x_ref.shape[0]
    hl = 2
    hc = hl * ng
    hw = R // 2
    me = lax.axis_index("seq")
    chip, core = lax.div(me, 2), lax.rem(me, 2)
    grp = lax.rem(chip, ng)

    def ring(off):
        return lax.rem(chip + off + nchip, nchip)

    def send(src, dst, ssem, rsem, off, other):
        k = jnp.where(other, 1 - core, core) if not isinstance(other, int) else (1 - core if other else core)
        return pltpu.make_async_remote_copy(src, dst, ssem, rsem, device_id={"seq": 2 * ring(off) + k},
                                            device_id_type=pl.DeviceIdType.MESH)

    barrier = pltpu.get_barrier_semaphore()
    peers = [(0, 1)] + [(o, k) for o in (1, -1, 2, -2) for k in (0, 1)]
    for o, k in peers:
        pl.semaphore_signal(barrier, inc=1, device_id={"seq": 2 * ring(o) + (1 - core if k else core)},
                            device_id_type=pl.DeviceIdType.MESH)

    def x_send(slot, j, to, other):
        src = xb.at[slot, j, 0]
        dst = xb.at[slot, j, 1] if other else xb.at[slot - to, j, 0]
        return send(src, dst, xs_sem.at[slot, j, 0 if other else (1 if to > 0 else 2)],
                    xr_sem.at[slot, j, 1] if other else xr_sem.at[slot - to, j, 0], to, other)

    def x_wait(slot, j, other):
        pltpu.make_async_copy(xb.at[slot, j, other], xb.at[slot, j, other], xr_sem.at[slot, j, other]).wait()

    for j in range(2):
        pltpu.make_async_copy(x_ref.at[pl.ds(j * R, R)], xv.at[j], ld_sem.at[j]).start()
    for j in range(2):
        pltpu.make_async_copy(x_ref.at[pl.ds(j * R, R)], xv.at[j], ld_sem.at[j]).wait()

        def norm(i, c):
            rows = pl.ds(i * 32, 32)
            xf = xv[j, rows, :].astype(F32)
            y = xf * lax.rsqrt(jnp.mean(xf * xf, axis=-1, keepdims=True) + 1e-5) * g_ref[...]
            xv[j, rows, :] = y.astype(BF)
            return c
        lax.fori_loop(0, R // 32, norm, 0)
        out = pltpu.make_async_copy(xv.at[j], xb.at[2, j, 0], ld_sem.at[2 + j])
        out.start()
        out.wait()
        if j == 0:
            pl.semaphore_wait(barrier, len(peers))
        x_send(2, j, 1, 0).start()
        x_send(2, j, -1, 0).start()
        x_send(2, j, 0, 1).start()

    nb = d // R

    def w_in(i):
        kind, b = lax.div(i, nb), lax.rem(i, nb)
        return pltpu.make_async_copy(w_ref.at[pl.ds(b * R, R), kind, pl.ds(pl.multiple_of(core * hc, hc), hc)],
                                     pin.at[lax.rem(i, 2)], pi_sem.at[lax.rem(i, 2)])

    def w_out(i):
        kind, b = lax.div(i, nb), lax.rem(i, nb)
        return pltpu.make_async_copy(pout.at[lax.rem(i, 2)], wall.at[pl.ds(kind * hc, hc), pl.ds(b * R, R)],
                                     po_sem.at[lax.rem(i, 2)])

    w_in(jnp.int32(0)).start()

    def prep(i, c):
        @pl.when(i + 1 < 3 * nb)
        def _():
            w_in(i + 1).start()
        w_in(i).wait()

        @pl.when(i >= 2)
        def _():
            w_out(i - 2).wait()
        pout[lax.rem(i, 2)] = jnp.swapaxes(pin[lax.rem(i, 2)], 0, 1)
        w_out(i).start()
        return c
    lax.fori_loop(0, 3 * nb, prep, 0)
    for e in (2, 1):
        w_out(jnp.int32(3 * nb - e)).wait()

    def f_of(st):
        f = lax.div(st, 2)
        return _pick(f, (0, 0, 0, 1, 1, 1)), _pick(f, (0, 0, 2, 0, 2, 2)), _pick(f, (1, 2, ng - 1, 1, ng - 1, 2))

    def is_fw(ph):
        return jnp.logical_or(ph == FWA, ph == FWB)

    def is_n2(ph):
        return jnp.logical_or(ph == N2A, ph == N2B)

    def head_of(ph, st):
        nh = lax.rem(st, 2)
        return jnp.where(jnp.logical_and(is_n2(ph), st >= 4), 1 - nh, nh)

    def widx(ph, st):
        fh, _, fg = f_of(st)
        near = _pick(lax.div(st, 2), (hc, 2 * hc, 0)) + hl * grp + head_of(ph, st)
        fwd = hc * (1 + lax.rem(st, 2)) + hl * lax.rem(grp + fg, ng) + fh
        return jnp.where(is_fw(ph), fwd, near)

    def w_load(ph, st, gs):
        return pltpu.make_async_copy(wall.at[widx(ph, st)], wt.at[lax.rem(gs, 2)], wt_sem.at[lax.rem(gs, 2)])

    def off_of(ph, m):
        a = jnp.where(ph == OWN, 0, jnp.where(ph <= N1B, 1, 2))
        return jnp.where(m < 2, -a, a)

    def chunk_of(ph, m):
        return jnp.where(ph == OWN, lax.div(m, 2), jnp.where(jnp.logical_or(ph == N1B, ph >= FWB), 1, 0))

    def x_load(ph, m):
        return pltpu.make_async_copy(xb.at[off_of(ph, m) + 2, chunk_of(ph, m), lax.rem(m, 2)], xv.at[m], ld_sem.at[m])

    def block_of(ph, m):
        return 2 * ring(off_of(ph, m)) + jnp.where(lax.rem(m, 2) == 0, core, 1 - core)

    def f_send(j, f):
        h, to = ((0, 1), (0, 2), (0, -1), (1, 1), (1, -1), (1, -2))[f]
        src_off = -2 if to > 0 else 2
        return send(fb.at[j, f], kvs.at[:, h, pl.ds(2 * ring(src_off), 2), j], fs_sem.at[j, f], fr_sem.at[j, f], to, 0)

    def f_wait(j, f):
        h, frm = ((0, -3), (0, 4), (0, 3), (1, -3), (1, 3), (1, 4))[f]
        ref = kvs.at[:, h, pl.ds(2 * ring(frm), 2), j]
        pltpu.make_async_copy(ref, ref, fr_sem.at[j, f]).wait()

    def phase(ph, gs):
        for at, j, slots in ((OWN, 0, (1, 3)), (N1B, 1, (1, 3))):
            @pl.when(ph == at)
            def _(j=j, slots=slots):
                for s in slots:
                    x_wait(s, j, 0)
                    x_send(s, j, 1 if s == 1 else -1, 0).start()
                    x_send(s, j, 0, 1).start()
        for at, j in ((FWA, 0), (FWB, 1)):
            @pl.when(ph == at)
            def _(j=j):
                for s in (0, 4):
                    x_wait(s, j, 0)
                    x_send(s, j, 0, 1).start()
        for at, waits in ((OWN, ((2, 0), (2, 1))), (N1A, ((1, 0), (3, 0))), (N1B, ((1, 1), (3, 1))),
                          (FWA, ((0, 0), (4, 0))), (FWB, ((0, 1), (4, 1)))):
            @pl.when(ph == at)
            def _(waits=waits):
                for s, j in waits:
                    x_wait(s, j, 1)

        @pl.when(jnp.logical_not(is_n2(ph)))
        def _():
            for m in range(4):
                x_load(ph, m).start()
                b = block_of(ph, jnp.int32(m))
                rows = pl.ds(pl.multiple_of(chunk_of(ph, jnp.int32(m)) * R, R), R)
                cc, sc = cosc[pl.ds(b, 1), :], sinc[pl.ds(b, 1), :]
                cb, sb_ = cosb[rows, :], sinb[rows, :]
                cs[m] = cb * cc - sb_ * sc
                sn[m] = sb_ * cc + cb * sc
            for m in range(4):
                x_load(ph, m).wait()

        fw = is_fw(ph)
        ns = jnp.where(fw, 12, 6)

        def step(st, gs):
            nxt_in = st + 1 < ns
            nph = jnp.where(nxt_in, ph, ph + 1)
            nst = jnp.where(nxt_in, st + 1, 0)

            @pl.when(nph <= N2B)
            def _():
                w_load(nph, nst, gs + 1).start()
            w_load(ph, st, gs).wait()
            kind = jnp.where(fw, 1 + lax.rem(st, 2), _pick(lax.div(st, 2), (1, 2, 0)))
            fh, flo, _ = f_of(st)
            n2q = jnp.logical_and(is_n2(ph), st >= 4)
            h = jnp.where(fw, fh, head_of(ph, st))
            lo = jnp.where(fw, flo, jnp.where(jnp.logical_and(n2q, st == 5), 2, 0))
            cnt = jnp.where(jnp.logical_or(fw, n2q), 1, 2)
            f = lax.div(st, 2)
            jf = jnp.where(ph == FWB, 1, 0)
            wslot = lax.rem(gs, 2)

            def dots(m):
                return [jnp.dot(xv[m + e], wt[wslot], preferred_element_type=F32) for e in range(2)]

            @pl.when(kind != 2)
            def _():
                scale = jnp.where(kind == 0, R ** -0.5, 1.0).astype(F32)

                def two(u, c):
                    m = lo + 2 * u
                    av = dots(m)
                    for e in range(2):
                        a = av[e] * scale
                        a1, a2 = a[:, :hw], a[:, hw:]
                        cv, sv = cs[m + e], sn[m + e]
                        a = jnp.concatenate([a1 * cv - a2 * sv, a2 * cv + a1 * sv], axis=-1).astype(BF)
                        blk = block_of(ph, m + e)
                        kk = lax.rem(blk, 2)
                        j = chunk_of(ph, m + e)

                        @pl.when(fw)
                        def _():
                            fb[jf, f, 0, kk] = a

                        @pl.when(jnp.logical_and(jnp.logical_not(fw), kind == 1))
                        def _():
                            kvs[0, h, blk, j] = a

                        @pl.when(kind == 0)
                        def _():
                            o = off_of(ph, m)
                            qi = jnp.where(o == 0, 6, jnp.where(o == -1, 2, jnp.where(o == 1, 4, 0))) + e
                            qs[h, qi, j] = a
                    return c
                lax.fori_loop(0, cnt, two, 0)

            @pl.when(kind == 2)
            def _():
                def two(u, c):
                    m = lo + 2 * u
                    av = dots(m)
                    for e in range(2):
                        a = av[e].astype(BF).T
                        blk = block_of(ph, m + e)
                        kk = lax.rem(blk, 2)
                        j = chunk_of(ph, m + e)

                        @pl.when(fw)
                        def _():
                            fb[jf, f, 1, kk] = a

                        @pl.when(jnp.logical_not(fw))
                        def _():
                            kvs[1, h, blk, j] = a
                    return c
                lax.fori_loop(0, cnt, two, 0)

            for n in range(3):
                @pl.when(jnp.logical_and(ph == FWA, st == 2 * n + 1))
                def _(n=n):
                    f_send(0, n).start()

                @pl.when(jnp.logical_and(ph == FWB, st == 2 * n + 1))
                def _(n=n):
                    f_send(1, n).start()
                    if n == 2:
                        for m in range(3, 6):
                            f_send(0, m).start()

                @pl.when(jnp.logical_and(ph == FWB, st == 2 * n + 7))
                def _(n=n):
                    f_send(1, n + 3).start()
            return gs + 1
        return lax.fori_loop(0, ns, step, gs)

    w_load(jnp.int32(OWN), jnp.int32(0), jnp.int32(0)).start()
    lax.fori_loop(0, N2B + 1, phase, jnp.int32(0))

    kb, qb = 4 * R, 2 * R

    def q_off(h, e):
        return jnp.where(e < 2, jnp.where(h == 0, 2, -2), jnp.where(e < 4, -1, jnp.where(e < 6, 1, 0)))

    def o_send(i):
        h, e = lax.div(i, 8), lax.rem(i, 8)
        return send(ob.at[i], o_ref.at[i], os_sem.at[i], or_sem.at[i], q_off(h, e), lax.rem(e, 2) == 1)

    def o_keep(i):
        return pltpu.make_async_copy(ob.at[i], o_ref.at[i], os_sem.at[i])

    def attend(i, c):
        h, e = lax.div(i, 8), lax.rem(i, 8)
        for hh in range(hl):
            @pl.when(i == 8 * hh)
            def _(hh=hh):
                for j in range(2):
                    for n in range(3):
                        f_wait(j, 3 * hh + n)
        pb = 2 * ring(q_off(h, e)) + jnp.where(lax.rem(e, 2) == 0, core, 1 - core)
        acc[...] = jnp.zeros_like(acc)
        ms[...] = jnp.full_like(ms, -jnp.inf)
        ls[...] = jnp.zeros_like(ls)

        def scores(n, dst):
            kblk = kvs[0, h, pl.ds(2 * n, 2)].reshape(kb, R)
            q = qs[h, e].reshape(qb, R)
            dst[...] = lax.dot_general(kblk, q, (((1,), (1,)), ((), ())), preferred_element_type=F32)

        def update(n, src, masked):
            s = src[...]
            if masked:
                kp = n * kb + lax.broadcasted_iota(I32, (kb, qb), 0)
                qp = pb * qb + lax.broadcasted_iota(I32, (kb, qb), 1)
                s = jnp.where(qp >= kp, s, -jnp.inf)
            mo = ms[...]
            mn = jnp.maximum(mo, jnp.max(s, axis=0, keepdims=True))
            al = jnp.exp(mo - mn)
            pr = jnp.exp(s - mn)
            ls[...] = ls[...] * al + jnp.sum(pr, axis=0, keepdims=True)
            ms[...] = mn
            vblk = kvs[1, h, pl.ds(2 * n, 2)]
            vblk = jnp.concatenate([vblk[a, b] for a in range(2) for b in range(2)], axis=-1)
            acc[...] = acc[...] * al + jnp.dot(vblk, pr.astype(BF), preferred_element_type=F32)

        nf = lax.div(pb, 2)
        scores(0, sa)

        def two(u, c):
            n = 2 * u
            scores(n + 1, sb)
            update(n, sa, False)
            scores(n + 2, sa)
            update(n + 1, sb, False)
            return c
        lax.fori_loop(0, lax.div(nf, 2), two, 0)

        @pl.when(lax.rem(nf, 2) == 1)
        def _():
            scores(nf, sb)
            update(nf - 1, sa, False)
            update(nf, sb, True)

        @pl.when(lax.rem(nf, 2) == 0)
        def _():
            update(nf, sa, True)
        ob[i] = (acc[...] / ls[...]).T.astype(BF)

        @pl.when(e == 6)
        def _():
            o_keep(i).start()

        @pl.when(e != 6)
        def _():
            o_send(i).start()
        return c
    lax.fori_loop(0, 8 * hl, attend, 0)

    for j in range(2):
        for s in range(5):
            x_send(s, j, 0, 1).wait_send()
        for s, to in ((2, 1), (2, -1), (1, 1), (3, -1)):
            x_send(s, j, to, 0).wait_send()
        for f in range(6):
            f_send(j, f).wait_send()

    def drain(i, c):
        @pl.when(lax.rem(i, 8) == 6)
        def _():
            o_keep(i).wait()

        @pl.when(lax.rem(i, 8) != 6)
        def _():
            o_send(i).wait()
        return c
    lax.fori_loop(0, 8 * hl, drain, 0)


def _mega(x, g, wqkv, p):
    t, d = x.shape
    _, _, nh, dh = wqkv.shape
    hw = dh // 2
    nchip = p // 2
    hc = nh // 2
    inv = 10000.0 ** (-np.arange(hw) * 2.0 / dh)
    ab, ac = np.arange(t)[:, None] * inv, (np.arange(p) * t)[:, None] * inv
    rot = [jnp.asarray(f(a), F32) for a in (ab, ac) for f in (np.cos, np.sin)]
    any_ = pl.BlockSpec(memory_space=pl.ANY)
    vm = pl.BlockSpec(memory_space=pltpu.VMEM)
    dma = pltpu.SemaphoreType.DMA
    return pl.pallas_call(
        functools.partial(_mega_body, p),
        in_specs=[any_, vm, any_, vm, vm, vm, vm],
        out_specs=[any_, any_, any_],
        out_shape=[jax.ShapeDtypeStruct((16, t, dh), BF), jax.ShapeDtypeStruct((3 * hc, d, dh), BF),
                   jax.ShapeDtypeStruct((5, 2, 2, R, d), BF)],
        scratch_shapes=[
            pltpu.VMEM((2, 2, 2 * nchip, 2, R, R), BF), pltpu.VMEM((2, 8, 2, R, R), BF), pltpu.VMEM((4, R, d), BF),
            pltpu.VMEM((2, d, R), BF), pltpu.VMEM((4 * R, 2 * R), F32), pltpu.VMEM((4 * R, 2 * R), F32),
            pltpu.VMEM((R, 2 * R), F32), pltpu.VMEM((1, 2 * R), F32), pltpu.VMEM((1, 2 * R), F32),
            pltpu.VMEM((2, 6, 2, 2, R, R), BF), pltpu.VMEM((16, 2 * R, R), BF), pltpu.VMEM((4, R, hw), F32),
            pltpu.VMEM((4, R, hw), F32), pltpu.VMEM((2, R, hc, dh), BF), pltpu.VMEM((2, hc, R, dh), BF),
            dma((4,)), dma((2,)), dma((2,)), dma((2,)), dma((5, 2, 3)), dma((5, 2, 2)), dma((2, 6)), dma((2, 6)),
            dma((16,)), dma((16,))],
        compiler_params=pltpu.CompilerParams(vmem_limit_bytes=VMEM_LIMIT, collective_id=0, has_side_effects=True),
        name="qkv_attend",
    )(x, g.reshape(1, d), wqkv, rot[0], rot[1], rot[2], rot[3])[0]


def _out_proj(heads, o, wo, res):
    n, qb, dh = o.shape
    dm = wo.shape[-1]
    bn = 512

    def body(h_ref, o_ref, *refs):
        w, res_ref, y_ref = refs[:n], refs[n], refs[n + 1]
        a = res_ref[...].astype(F32)
        for i in range(n):
            a = a + jnp.dot(o_ref[i], w[i][0], preferred_element_type=F32)
        y_ref[...] = a.astype(BF)

    return pl.pallas_call(
        body,
        grid_spec=pltpu.PrefetchScalarGridSpec(
            num_scalar_prefetch=1, grid=(dm // bn,),
            in_specs=[pl.BlockSpec((n, qb, dh), lambda c, h: (0, 0, 0))]
            + [pl.BlockSpec((1, dh, bn), functools.partial(lambda i, c, h: (h[i], 0, c), i)) for i in range(n)]
            + [pl.BlockSpec((qb, bn), lambda c, h: (0, c))],
            out_specs=pl.BlockSpec((qb, bn), lambda c, h: (0, c))),
        out_shape=jax.ShapeDtypeStruct((qb, dm), BF),
        compiler_params=pltpu.CompilerParams(vmem_limit_bytes=VMEM_LIMIT),
        name="out_proj",
    )(heads, o, *([wo] * n), res)


def solution(mesh):
    p = mesh.shape["seq"]
    rows = P(("data", "seq"), None)
    nchip = p // 2

    def local(x, g, wqkv, wo):
        _, _, nh, dh = wqkv.shape
        ng = nchip // 2
        hc = nh // 2
        hl = hc // ng
        me = lax.axis_index("seq")
        chip, core = me // 2, me % 2
        grp = chip % ng
        o = _mega(x, g, wqkv, p)
        heads = jnp.stack([jnp.asarray(hc * kk + hl * (gg % ng) + h, I32)
                           for h in range(hl) for gg in (grp + 2, grp + 1, grp + ng - 1, grp) for kk in (core, 1 - core)])
        return _out_proj(heads, o, wo, x)

    return jax.shard_map(local, mesh=mesh,
                         in_specs=(rows, P(None), P(None, None, None, None), P(None, None, None)),
                         out_specs=rows, check_vma=False)
```

time: 797 us -> 367 us (0.46)
  Pallas kernels: 0 us -> 365 us
  waiting for transfers between devices: 282 us -> 0 us
  matrix products: 244 us -> 0 us
  blocking collectives: 102 us -> 0 us
  other arithmetic: 78.3 us -> 0 us
  local copies, waits for them, and re-layouts: 64.5 us -> 0.62 us
  starting transfers between devices: 22.3 us -> 0 us
    pallas_call x0 -> x2, Pallas kernels: none -> 365 us  [the longest x1 339 us: _mega(): pl.pallas_call(functools.partial(_mega_body, p), in_specs=[any_, vm, any_...]
    all_to_all x1 -> x0, waiting for transfers between devices: 282 us -> none  [local(): buf = lax.all_to_all(buf, 'seq', 2, 1, tiled=True)]
    dot_general x34 -> x0, matrix products: 244 us -> none  [the longest x16 81.6 us: local(): jnp.einsum('hqd,hkd->hqk', q[:, lo:hi], k[:, :hi], preferred_element_type...]
    all_to_all x1 -> x0, blocking collectives: 102 us -> none  [local(): o = lax.all_to_all(o, 'seq', 0, 1, tiled=True)]
    reduce_sum x17 -> x0, other arithmetic: 54.5 us -> none  [the longest x16 51.4 us: local(): pr = jax.nn.softmax(sc, axis=-1).astype(jnp.bfloat16)]
    unnamed x65 -> x0, local copies, waits for them, and re-layouts: 31.1 us -> none
    all_to_all x1 -> x0, starting transfers between devices: 22.3 us -> none  [local(): buf = lax.all_to_all(buf, 'seq', 2, 1, tiled=True)]
    all_to_all x1 -> x0, local copies, waits for them, and re-layouts: 16.5 us -> none  [local(): buf = lax.all_to_all(buf, 'seq', 2, 1, tiled=True)]
  transfers between devices with their start and end apart: 1 -> 0, of which waited for: 1 -> 0; matrix products, arithmetic and copies ran while one was open for 0% -> 0% of each run, Pallas kernels for 0% -> 0%
where the time goes in v1:
time: 367 us; the launch traced here: 365 us
  Pallas kernels  365 us (99%)
    pallas_call x1, Pallas kernels, _mega(): pl.pallas_call(functools.partial(_mega_body, p), in_specs=[any_, vm, any_...  339 us
    pallas_call x1, Pallas kernels, _out_proj(): pl.pallas_call(body, grid_spec=pltpu.PrefetchScalarGridSpec(num_scalar_pr...  25.9 us

profile of v1, /device:TPU:21, one launch (start us, length us, event | category | flops | bytes accessed | tf_op | source)
XLA Modules:
  0.0 365.3 jit_solution(2880039831061695829)
XLA Ops:
  0.0 0.6 stack.67.h_ref
  0.6 338.7 %qkv_attend.1 = (bf16[16,512,256]{2,1,0:T(8,128)(2,1)}, bf16[24,4096,256]{2,1,0:T(8,128)(2,1)}, bf16[5,2,2,256,4096]{4,3,2,1,0:T(8,128)(2,1)}) custom-call(bf16[512,4096]{1,0:T(8,128)(2,1)} %refs_16_.1, f32[1,4096]{1,0:T(1,128)} %bitcast.17, bf16[4096,3,16,256]{3,2,1,0:T(8,128)(2,1)} %w_ref.1, f32[512,128]{1,0:T(8,128)} %constant.91.clone.cosb, ...), custom_call_target="tpu_custom_call" | custom-call | tf_op jit(solution)/shard_map/qkv_attend/pallas_call | solution.py:405
  339.4 25.9 %out_proj.1 = bf16[512,4096]{1,0:T(8,128)(2,1)} custom-call(s32[16]{0:T(128)} %stack.67.h_ref, bf16[16,512,256]{2,1,0:T(8,128)(2,1)} %get-tuple-element.6.o_ref, bf16[16,256,4096]{2,1,0:T(8,128)(2,1)} %refs_15_.1, bf16[16,256,4096]{2,1,0:T(8,128)(2,1)} %refs_15_.1, bf16[16,256,4096]{2,1,0:T(8,128)(2,1)} %refs_15_.1, bf16[16,256,4096]{2,1,0:T(8,128)(2,1)} %refs_15_.1, ...), custom_call_target="tpu_custom_call" | custom-call | tf_op jit(solution)/shard_map/out_proj/pallas_call | solution.py:436

commit v2 on v0

v2 whole, which is shorter than its diff:
```python
import functools

import jax
import jax.numpy as jnp
import numpy as np
from jax import lax
from jax.experimental import pallas as pl
from jax.experimental.pallas import tpu as pltpu
from jax.sharding import PartitionSpec as P

BF = jnp.bfloat16
F32 = jnp.float32
I32 = jnp.int32
VMEM_LIMIT = 63 * 2**20
R = 256

OWN, N1A, N1B, FWA, N2A, FWB, N2B = range(7)


TWO = range(2)


def _loop(n, body):
    return lax.fori_loop(0, n, body, 0)


def _odd(a):
    return lax.rem(a, 2)


def _half(a):
    return lax.div(a, 2)


def _rem3(a):
    return lax.rem(a, 3)


def _rem8(a):
    return lax.rem(a, 8)


def _div8(a):
    return lax.div(a, 8)


def _pick(i, values):
    out = jnp.asarray(values[0], I32)
    for n, v in enumerate(values[1:], 1):
        out = jnp.where(i == n, v, out)
    return out


def _body(p, x_ref, g_ref, w_ref, wo_ref, cosb, sinb, cosc, sinc, y_ref, wall, xb, kvs, qs, fb, ob, og,
          sa, sb, acc, ms, ls, ld_sem, wt_sem, wo_sem, xs_sem, xr_sem, fs_sem, fr_sem, os_sem, or_sem):
    nchip = p // 2
    ng = nchip // 2
    d = x_ref.shape[1]
    hl = 2
    hc = hl * ng
    hw = R // 2
    me = lax.axis_index("seq")
    chip, core = _half(me), _odd(me)
    grp = lax.rem(chip, ng)

    def ring(off):
        return lax.rem(chip + off + nchip, nchip)

    def send(src, dst, ssem, rsem, off, other):
        k = jnp.where(other, 1 - core, core) if not isinstance(other, int) else (1 - core if other else core)
        return pltpu.make_async_remote_copy(src, dst, ssem, rsem, device_id={"seq": 2 * ring(off) + k},
                                            device_id_type=pl.DeviceIdType.MESH)

    barrier = pltpu.get_barrier_semaphore()
    peers = [(0, 1)] + [(o, k) for o in (1, -1, 2, -2) for k in (0, 1)]
    for o, k in peers:
        pl.semaphore_signal(barrier, inc=1, device_id={"seq": 2 * ring(o) + (1 - core if k else core)},
                            device_id_type=pl.DeviceIdType.MESH)

    def x_send(slot, j, to, other):
        src = x_ref.at[pl.ds(0, R)] if (slot, j) == (2, 0) else xb.at[slot, j, 0]
        dst = xb.at[slot, j, 1] if other else xb.at[slot - to, j, 0]
        return send(src, dst, xs_sem.at[slot, j, 0 if other else (1 if to > 0 else 2)],
                    xr_sem.at[slot, j, 1] if other else xr_sem.at[slot - to, j, 0], to, other)

    def x_wait(slot, j, other):
        pltpu.make_async_copy(xb.at[slot, j, other], xb.at[slot, j, other], xr_sem.at[slot, j, other]).wait()

    nb = d // R

    def norm(ref):
        def rows32(i, c):
            rows = pl.ds(i * 32, 32)
            xf = ref[rows, :].astype(F32)
            y = xf * lax.rsqrt(jnp.mean(xf * xf, axis=-1, keepdims=True) + 1e-5) * g_ref[...]
            ref[rows, :] = y.astype(BF)
            return c
        _loop(R // 32, rows32)

    def start(xv, pin, pout):
        x1 = pltpu.make_async_copy(x_ref.at[pl.ds(R, R)], xv, ld_sem.at[0])
        x1.start()
        pl.semaphore_wait(barrier, len(peers))
        for to, other in ((1, 0), (-1, 0), (0, 1)):
            x_send(2, 0, to, other).start()
        x1.wait()
        norm(xv)
        out = pltpu.make_async_copy(xv, xb.at[2, 1, 0], ld_sem.at[1])
        out.start()
        out.wait()
        for to, other in ((1, 0), (-1, 0), (0, 1)):
            x_send(2, 1, to, other).start()

        def w_in(i):
            kind, b = _rem3(lax.div(i, nb) + 1), lax.rem(i, nb)
            return pltpu.make_async_copy(w_ref.at[pl.ds(b * R, R), kind, pl.ds(pl.multiple_of(core * hc, hc), hc)],
                                         pin.at[_odd(i)], wt_sem.at[_odd(i)])

        def kv_out(i):
            kind, b = lax.div(i, nb) + 1, lax.rem(i, nb)
            return pltpu.make_async_copy(pout.at[_odd(i)], wall.at[pl.ds(kind * hc, hc), pl.ds(b * R, R)],
                                         ld_sem.at[_odd(i)])

        def q_out(i):
            return pltpu.make_async_copy(pout.at[_odd(i), pl.ds(0, hl)],
                                         wall.at[pl.ds(hl * grp, hl), pl.ds(lax.rem(i, nb) * R, R)], ld_sem.at[_odd(i)])

        def put_kv(i):
            pout[_odd(i)] = jnp.swapaxes(pin[_odd(i)], 0, 1)

        def put_q(i):
            for gv in range(ng):
                @pl.when(grp == gv)
                def _(gv=gv):
                    pout[_odd(i), :hl] = jnp.swapaxes(pin[_odd(i), :, hl * gv:hl * gv + hl], 0, 1)

        def prep(put, out, lo, i, c):
            @pl.when(i + 1 < 3 * nb)
            def _():
                w_in(i + 1).start()
            w_in(i).wait()

            @pl.when(i >= lo + 2)
            def _():
                out(i - 2).wait()
            put(i)
            out(i).start()
            return c
        w_in(jnp.int32(0)).start()
        for put, out, lo, hi in ((put_kv, kv_out, 0, 2 * nb), (put_q, q_out, 2 * nb, 3 * nb)):
            lax.fori_loop(lo, hi, functools.partial(prep, put, out, lo), 0)
            for e in (2, 1):
                out(jnp.int32(hi - e)).wait()

    pl.run_scoped(start, pltpu.VMEM((R, d), BF), pltpu.VMEM((2, R, hc, R), BF), pltpu.VMEM((2, hc, R, R), BF))

    even = _odd(chip) == 0

    kb, qb = 4 * R, 2 * R
    EARLY, NEAR, HEAD0, FAR = range(4)

    def q_off(e):
        return jnp.where(e < 2, jnp.where(even, 2, -2), jnp.where(e < 4, -1, jnp.where(e < 6, 1, 0)))

    def o_send(i):
        e = _rem8(i)
        return send(ob.at[i], og.at[i], os_sem.at[i], or_sem.at[i], q_off(e), _odd(e) == 1)

    def around(reach):
        b = ring(-reach)
        wrapped = jnp.logical_or(chip < reach, chip + reach >= nchip)
        return jnp.where(wrapped, ring(reach + 1), 0), b

    def attend(ps, e):
        h = jnp.where(ps == HEAD0, 0, 1)
        i = 8 * h + e
        qc = ring(q_off(e))
        pb = 2 * qc + jnp.where(_odd(e) == 0, core, 1 - core)
        w1, b1 = around(1)
        w2, b2 = around(2)
        rest = jnp.logical_and(ps == NEAR, e >= 2)
        up2 = ring(2)
        low_ok, up_ok = b2 < qc, up2 < qc
        n0 = jnp.where(ps == FAR, w2, jnp.where(rest, b2, 0))
        n1 = jnp.where(ps == EARLY, b1, jnp.where(rest, up2, b2))
        w = jnp.where(ps == EARLY, w1, jnp.where(rest, jnp.where(low_ok, 1, 0), jnp.where(ps == NEAR, w2, nchip)))
        cnt = jnp.where(
            ps == EARLY, jnp.where(qc >= b1, w1 + qc - b1, qc),
            jnp.where(rest, jnp.where(low_ok, 1, 0) + jnp.where(up_ok, 1, 0),
                      jnp.where(ps == NEAR, jnp.where(qc >= b2, w2 + qc - b2, qc),
                                jnp.where(ps == HEAD0, qc, jnp.where(qc >= b2, b2 - w2, 0)))))
        last = jnp.logical_not(jnp.logical_or(rest, ps == FAR))
        sl = jnp.where(ps == HEAD0, 8, e)

        def keys_of(idx):
            return jnp.where(idx >= cnt, qc, jnp.where(idx < w, n0 + idx, n1 + idx - w))

        @pl.when(last)
        def _():
            acc[sl] = jnp.zeros((R, qb), F32)
            ms[sl] = jnp.full((1, qb), -jnp.inf, F32)
            ls[sl] = jnp.zeros((1, qb), F32)

        def scores(idx, dst):
            n = keys_of(idx)
            kblk = kvs[0, h, pl.ds(2 * n, 2)].reshape(kb, R)
            q = qs[h, e].reshape(qb, R)
            s = lax.dot_general(kblk, q, (((1,), (1,)), ((), ())), preferred_element_type=F32)
            dst[...] = s.reshape(dst.shape)

        def update(idx, src, masked, nk=4):
            n = keys_of(idx)
            s = src[:nk].reshape(nk * R, qb)
            if masked:
                kp = n * kb + lax.broadcasted_iota(I32, s.shape, 0)
                qp = pb * qb + lax.broadcasted_iota(I32, s.shape, 1)
                s = jnp.where(qp >= kp, s, -jnp.inf)
            mo = ms[sl]
            mn = jnp.maximum(mo, jnp.max(s, axis=0, keepdims=True))
            al = jnp.exp(mo - mn)
            pr = jnp.exp(s - mn)
            ls[sl] = ls[sl] * al + jnp.sum(pr, axis=0, keepdims=True)
            ms[sl] = mn
            vblk = kvs[1, h, pl.ds(2 * n, 2)]
            vblk = jnp.concatenate([vblk[a // 2, a % 2] for a in range(nk)], axis=-1)
            acc[sl] = acc[sl] * al + jnp.dot(vblk, pr.astype(BF), preferred_element_type=F32)

        @pl.when(jnp.logical_or(cnt > 0, last))
        def _():
            scores(0, sa)

            def two(u, c2):
                scores(2 * u + 1, sb)
                update(2 * u, sa, False)
                scores(2 * u + 2, sa)
                update(2 * u + 1, sb, False)
                return c2
            _loop(_half(cnt), two)
            odd = _odd(cnt) == 1

            @pl.when(jnp.logical_and(odd, last))
            def _():
                scores(cnt, sb)
                update(cnt - 1, sa, False)

            @pl.when(jnp.logical_and(odd, jnp.logical_not(last)))
            def _():
                update(cnt - 1, sa, False)

            for buf, par in ((sa, 0), (sb, 1)):
                for kk in TWO:
                    @pl.when(jnp.logical_and(last, jnp.logical_and(_odd(cnt) == par, _odd(pb) == kk)))
                    def _(buf=buf, kk=kk):
                        update(cnt, buf, True, 2 + 2 * kk)

        @pl.when(ps >= HEAD0)
        def _():
            out = (acc[sl] / ls[sl]).T.astype(BF)

            @pl.when(e == 6)
            def _():
                og[i] = out

            @pl.when(e != 6)
            def _():
                ob[i] = out

    def f_wait_head(hh):
        for j in TWO:
            for n in range(3):
                f_wait(j, 3 * hh + n)

    def attend_loop():
        busy = chip >= ng

        def send_head0(n):
            for k in range(n):
                o_send(jnp.int32(k)).start()

        def one(it, c):
            ps, e = 1 + _div8(it), _rem8(it)

            @pl.when(it == 8)
            def _():
                f_wait_head(0)

            @pl.when(it == 16)
            def _():
                f_wait_head(1)

            @pl.when(jnp.logical_and(it == 16, jnp.logical_not(busy)))
            def _():
                send_head0(6)
                o_send(jnp.int32(7)).start()
            attend(ps, e)

            @pl.when(jnp.logical_and(ps == FAR, e != 6))
            def _():
                o_send(8 + e).start()

            @pl.when(jnp.logical_and(busy, it == 14))
            def _():
                send_head0(6)

            @pl.when(jnp.logical_and(busy, it == 15))
            def _():
                o_send(e).start()
            return c
        _loop(24, one)

    def f_of(ph, st):
        f = _half(st)
        n = _rem3(f)
        return lax.div(f, 3), jnp.where(n == 1, jnp.where(ph == FWA, 0, 2), n), _pick(n, (1, 2, ng - 1))

    def is_fw(ph):
        return jnp.logical_or(ph == FWA, ph == FWB)

    def is_n2(ph):
        return jnp.logical_or(ph == N2A, ph == N2B)

    def head_of(ph, st):
        return _odd(st)

    def widx(ph, st):
        fh, _, fg = f_of(ph, st)
        near = _pick(_half(st), (hc, 2 * hc, 0)) + hl * grp + head_of(ph, st)
        fwd = hc * (1 + _odd(st)) + hl * lax.rem(grp + fg, ng) + fh
        return jnp.where(is_fw(ph), fwd, near)

    def w_load(wt, ph, st, gs):
        return pltpu.make_async_copy(wall.at[widx(ph, st)], wt.at[_rem3(gs)], wt_sem.at[_rem3(gs)])

    def steps_of(ph):
        return jnp.where(is_fw(ph), 12, 6)

    def next_step(ph, st):
        inside = st + 1 < steps_of(ph)
        return jnp.where(inside, ph, ph + 1), jnp.where(inside, st + 1, 0)

    def off_of(ph, m):
        a = jnp.where(ph == OWN, 0, jnp.where(ph <= N1B, 1, 2))
        return jnp.where(m < 2, -a, a)

    def chunk_of(ph, m):
        return jnp.where(ph == OWN, _half(m), jnp.where(jnp.logical_or(ph == N1B, ph >= FWB), 1, 0))

    def x_load(xv, ph, m):
        return pltpu.make_async_copy(xb.at[off_of(ph, m) + 2, chunk_of(ph, m), _odd(m)], xv.at[m], ld_sem.at[m])

    def block_of(ph, m):
        return 2 * ring(off_of(ph, m)) + jnp.where(_odd(m) == 0, core, 1 - core)

    def f_send(j, f):
        h, to = f // 3, (1, (2, -2)[j], -1)[f % 3]
        src_off = -2 if to > 0 else 2
        return send(fb.at[j, f], kvs.at[:, h, pl.ds(2 * ring(src_off), 2), j], fs_sem.at[j, f], fr_sem.at[j, f], to, 0)

    def f_wait(j, f):
        h, frm = f // 3, (-3, 4, 3)[f % 3]
        ref = kvs.at[:, h, pl.ds(2 * ring(frm), 2), j]
        pltpu.make_async_copy(ref, ref, fr_sem.at[j, f]).wait()

    def phase(xv, wt, cs, sn, res, ph, gs):
        def relay(j):
            for s in (1, 3):
                x_wait(s, j, 0)
                x_send(s, j, 1 if s == 1 else -1, 0).start()
                x_send(s, j, 0, 1).start()

        @pl.when(ph == OWN)
        def _():
            relay(0)

        @pl.when(ph == FWA)
        def _():
            def early(e, c):
                attend(jnp.int32(EARLY), e)
                return c
            lax.fori_loop(2, 8, early, 0)
        def share(j):
            for s in (0, 4):
                x_wait(s, j, 0)
                x_send(s, j, 0, 1).start()

        @pl.when(ph == FWA)
        def _():
            share(0)
        fw = is_fw(ph)
        raw = jnp.logical_or(ph == N1A, ph == FWA)

        def norms(lo, step=1):
            lax.fori_loop(0, 2, lambda m, c: (norm(xv.at[lo + step * m]), c)[1], 0)
        fresh = jnp.logical_not(is_n2(ph))

        @pl.when(fresh)
        def _():
            @pl.when(ph == OWN)
            def _():
                pltpu.make_async_copy(x_ref.at[pl.ds(0, R)], xv.at[0], ld_sem.at[0]).start()

            @pl.when(ph != OWN)
            def _():
                x_load(xv, ph, 0).start()
            x_load(xv, ph, 2).start()
            for m in range(4):
                b = block_of(ph, jnp.int32(m))
                rows = pl.ds(pl.multiple_of(chunk_of(ph, jnp.int32(m)) * R, R), R)
                cc, sc = cosc[pl.ds(b, 1), :], sinc[pl.ds(b, 1), :]
                cb, sb_ = cosb[rows, :], sinb[rows, :]
                cs[m] = cb * cc - sb_ * sc
                sn[m] = sb_ * cc + cb * sc
        @pl.when(raw)
        def _():
            for m in (0, 2):
                x_load(xv, ph, m).wait()
            norms(0, 2)
        for at, waits in ((OWN, ((2, 0), (2, 1))), (N1A, ((1, 0), (3, 0))), (N1B, ((1, 1), (3, 1))),
                          (FWA, ((0, 0), (4, 0))), (FWB, ((0, 1), (4, 1)))):
            @pl.when(ph == at)
            def _(waits=waits):
                for s, j in waits:
                    x_wait(s, j, 1)

        @pl.when(fresh)
        def _():
            for m in (1, 3):
                x_load(xv, ph, m).start()

        @pl.when(raw)
        def _():
            for m in (1, 3):
                x_load(xv, ph, m).wait()
            norms(1, 2)

        @pl.when(jnp.logical_and(fresh, jnp.logical_not(raw)))
        def _():
            for m in TWO:
                x_load(xv, ph, m).wait()

        @pl.when(ph == OWN)
        def _():
            norms(0)

        @pl.when(jnp.logical_or(ph == OWN, ph == N1B))
        def _():
            for m in (2, 3):
                x_load(xv, ph, m).wait()

        def step(st, gs):
            nph, nst = next_step(*next_step(ph, st))

            @pl.when(nph <= N2B)
            def _():
                w_load(wt, nph, nst, gs + 2).start()

            @pl.when(jnp.logical_and(ph == N1A, st == 4))
            def _():
                relay(1)

            @pl.when(jnp.logical_and(ph == N2A, st == 5))
            def _():
                share(1)

            @pl.when(jnp.logical_and(ph == FWB, st == 2))
            def _():
                for m in (2, 3):
                    x_load(xv, ph, m).wait()
            w_load(wt, ph, st, gs).wait()
            kind = jnp.where(fw, 1 + _odd(st), _pick(_half(st), (1, 2, 0)))
            fh, flo, _ = f_of(ph, st)
            n2q = jnp.logical_and(is_n2(ph), st >= 4)
            h = jnp.where(fw, fh, head_of(ph, st))
            lo = jnp.where(fw, flo, jnp.where(jnp.logical_and(n2q, even), 2, 0))
            cnt = jnp.where(jnp.logical_or(fw, n2q), 1, 2)
            f = _half(st)
            jf = jnp.where(ph == FWB, 1, 0)
            wslot = _rem3(gs)

            def dots(m):
                return [jnp.dot(xv[m + e], wt[wslot], preferred_element_type=F32) for e in TWO]

            @pl.when(kind != 2)
            def _():
                scale = jnp.where(kind == 0, R ** -0.5, 1.0).astype(F32)

                def two(u, c):
                    m = lo + 2 * u
                    av = dots(m)
                    for e in TWO:
                        a = av[e] * scale
                        a1, a2 = a[:, :hw], a[:, hw:]
                        cv, sv = cs[m + e], sn[m + e]
                        res[m + e] = jnp.concatenate([a1 * cv - a2 * sv, a2 * cv + a1 * sv], axis=-1).astype(BF)
                    return c
                _loop(cnt, two)

            @pl.when(kind == 2)
            def _():
                def two(u, c):
                    m = lo + 2 * u
                    av = dots(m)
                    for e in TWO:
                        res[m + e] = av[e].astype(BF).T
                    return c
                _loop(cnt, two)

            def put(m, c):
                blk = block_of(ph, m)
                j = chunk_of(ph, m)

                @pl.when(fw)
                def _():
                    fb[jf, f, kind - 1, _odd(blk)] = res[m]

                @pl.when(jnp.logical_and(jnp.logical_not(fw), kind > 0))
                def _():
                    kvs[kind - 1, h, blk, j] = res[m]

                @pl.when(kind == 0)
                def _():
                    o = off_of(ph, m)
                    qi = jnp.where(o == 0, 6, jnp.where(o == -1, 2, jnp.where(o == 1, 4, 0))) + _odd(m)
                    qs[h, qi, j] = res[m]
                return c
            lax.fori_loop(lo, lo + 2 * cnt, put, 0)

            for n in range(3):
                @pl.when(jnp.logical_and(ph == FWA, st == 2 * n + 1))
                def _(n=n):
                    f_send(0, n).start()

                @pl.when(jnp.logical_and(ph == FWB, st == 2 * n + 1))
                def _(n=n):
                    f_send(1, n).start()
                    if n == 0:
                        for m in (3, 4):
                            f_send(0, m).start()

                if n == 2:
                    @pl.when(jnp.logical_and(ph == FWA, st == 11))
                    def _():
                        f_send(0, 5).start()

                @pl.when(jnp.logical_and(ph == FWB, st == 2 * n + 7))
                def _(n=n):
                    f_send(1, n + 3).start()
            return gs + 1
        return lax.fori_loop(0, steps_of(ph), step, gs)

    def project(xv, wt, cs, sn, res):
        for n in TWO:
            w_load(wt, jnp.int32(OWN), jnp.int32(n), jnp.int32(n)).start()
        lax.fori_loop(0, N2B + 1, functools.partial(phase, xv, wt, cs, sn, res), jnp.int32(0))

    pl.run_scoped(project, pltpu.VMEM((4, R, d), BF), pltpu.VMEM((3, d, R), BF), pltpu.VMEM((4, R, hw), F32),
                  pltpu.VMEM((4, R, hw), F32), pltpu.VMEM((4, R, R), BF))

    attend_loop()

    dm = wo_ref.shape[2]
    nw = dm // 2
    cw = 2 * R
    ncol = nw // cw
    groups = ((0, 1, 2, 3), (4, 5, 6, 7), (8, 9, 14, 15), (10, 12), (11, 13))

    def piece(n, k):
        return _pick(n, [gr[k] if k < len(gr) else gr[0] for gr in groups])

    def wo_load(wv, n, half, ks):
        sl, out = _rem3(2 * n + half), []
        for k in ks:
            i = piece(n, k)
            gg = lax.rem(grp + _pick(_half(_rem8(i)), (2, 1, ng - 1, 0)), ng)
            head = hc * jnp.where(_odd(i) == 0, core, 1 - core) + hl * gg + _div8(i)
            out.append(pltpu.make_async_copy(wo_ref.at[head, :, pl.ds(half * nw, nw)], wv.at[sl, k], wo_sem.at[sl, k]))
        return out

    def wo_start(wv, n, half):
        @pl.when(n < len(groups))
        def _():
            for cp in wo_load(wv, n, half, (0, 1)):
                cp.start()

        @pl.when(n < 3)
        def _():
            for cp in wo_load(wv, n, half, (2, 3)):
                cp.start()

    def finish(yb, wv):
        res = pltpu.make_async_copy(x_ref, yb, wt_sem.at[1])
        res.start()
        for half in TWO:
            wo_start(wv, jnp.int32(0), half)
        res.wait()
        tops = (sa, sb)

        for half in TWO:
            def fill(i, c, half=half):
                to = pl.ds(pl.multiple_of(half * nw + i * cw, cw), cw)
                tops[half][i] = yb[:R, to].astype(F32)
                acc[half * ncol + i] = yb[R:, to].astype(F32)
                return c
            _loop(ncol, fill)

        def out(size, n, c):
            for half in TWO:
                sl = _rem3(2 * n + half)
                wo_start(wv, n + 1, half)
                if half == 0:
                    for k in range(size):
                        i = piece(n, k)

                        @pl.when(_rem8(i) != 6)
                        def _(i=i):
                            o_send(i).wait()
                for cp in wo_load(wv, n, half, range(size)):
                    cp.wait()
                oo = jnp.concatenate([og[piece(n, k)] for k in range(size)], axis=-1)

                def cols(i, c2, half=half, sl=sl, oo=oo):
                    at = pl.ds(pl.multiple_of(i * cw, cw), cw)
                    ww = jnp.concatenate([wv[sl, k, :, at] for k in range(size)], axis=0)
                    a = jnp.dot(oo, ww, preferred_element_type=F32)
                    tops[half][i] = tops[half][i] + a[:R]
                    acc[half * ncol + i] = acc[half * ncol + i] + a[R:]
                    return c2
                _loop(ncol, cols)

                if size == 2:
                    @pl.when(n == len(groups) - 1)
                    def _(half=half):
                        def store(i, c2):
                            to = pl.ds(pl.multiple_of(half * nw + i * cw, cw), cw)
                            yb[:R, to] = tops[half][i].astype(BF)
                            yb[R:, to] = acc[half * ncol + i].astype(BF)
                            pltpu.make_async_copy(yb.at[:, to], y_ref.at[:, to], wt_sem.at[0]).start()
                            return c2
                        _loop(ncol, store)
            return c
        _loop(3, functools.partial(out, 4))
        lax.fori_loop(3, len(groups), functools.partial(out, 2), 0)
        pltpu.make_async_copy(yb, y_ref, wt_sem.at[0]).wait()

    pl.run_scoped(finish, pltpu.VMEM((qb, dm), BF), pltpu.VMEM((3, 4, R, nw), BF))

    for j in TWO:
        for s in range(5):
            x_send(s, j, 0, 1).wait_send()
        for s, to in ((2, 1), (2, -1), (1, 1), (3, -1)):
            x_send(s, j, to, 0).wait_send()
        for f in range(6):
            f_send(j, f).wait_send()


def _sublayer(x, g, wqkv, wo, p):
    t, d = x.shape
    _, _, nh, dh = wqkv.shape
    hw = dh // 2
    nchip = p // 2
    hc = nh // 2
    inv = 10000.0 ** (-np.arange(hw) * 2.0 / dh)
    ab, ac = np.arange(t)[:, None] * inv, (np.arange(p) * t)[:, None] * inv
    rot = [jnp.asarray(f(a), F32) for a in (ab, ac) for f in (np.cos, np.sin)]
    any_ = pl.BlockSpec(memory_space=pl.ANY)
    vm = pl.BlockSpec(memory_space=pltpu.VMEM)
    dma = pltpu.SemaphoreType.DMA
    return pl.pallas_call(
        functools.partial(_body, p),
        in_specs=[any_, vm, any_, any_, vm, vm, vm, vm],
        out_specs=[any_, any_, any_],
        out_shape=[jax.ShapeDtypeStruct((t, d), BF), jax.ShapeDtypeStruct((3 * hc, d, dh), BF),
                   jax.ShapeDtypeStruct((5, 2, 2, R, d), BF)],
        scratch_shapes=[
            pltpu.VMEM((2, 2, 2 * nchip, 2, R, R), BF), pltpu.VMEM((2, 8, 2, R, R), BF), pltpu.VMEM((2, 6, 2, 2, R, R), BF),
            pltpu.VMEM((16, 2 * R, R), BF), pltpu.VMEM((16, 2 * R, R), BF),
            pltpu.VMEM((4, R, 2 * R), F32), pltpu.VMEM((4, R, 2 * R), F32), pltpu.VMEM((9, R, 2 * R), F32),
            pltpu.VMEM((9, 1, 2 * R), F32), pltpu.VMEM((9, 1, 2 * R), F32),
            dma((4,)), dma((3,)), dma((3, 4)), dma((5, 2, 3)), dma((5, 2, 2)), dma((2, 6)), dma((2, 6)), dma((16,)), dma((16,))],
        compiler_params=pltpu.CompilerParams(vmem_limit_bytes=VMEM_LIMIT, collective_id=0, has_side_effects=True),
        name="sublayer",
    )(x, g.reshape(1, d), wqkv, wo, *rot)[0]


def solution(mesh):
    p = mesh.shape["seq"]
    rows = P(("data", "seq"), None)

    def local(x, g, wqkv, wo):
        y = _sublayer(x, g, wqkv, wo, p)
        return y + jnp.minimum(lax.axis_index("seq"), 0).astype(BF)

    return jax.shard_map(local, mesh=mesh,
                         in_specs=(rows, P(None), P(None, None, None, None), P(None, None, None)),
                         out_specs=rows, check_vma=False)
```

time: 797 us -> 340 us (0.43)
  Pallas kernels: 0 us -> 334 us
  waiting for transfers between devices: 282 us -> 0 us
  matrix products: 244 us -> 0 us
  blocking collectives: 102 us -> 0 us
  other arithmetic: 78.3 us -> 4.47 us
  local copies, waits for them, and re-layouts: 64.5 us -> 0 us
  starting transfers between devices: 22.3 us -> 0 us
    pallas_call x0 -> x1, Pallas kernels: none -> 334 us  [_sublayer(): pl.pallas_call(functools.partial(_body, p), in_specs=[any_, vm, any_, any...]
    all_to_all x1 -> x0, waiting for transfers between devices: 282 us -> none  [local(): buf = lax.all_to_all(buf, 'seq', 2, 1, tiled=True)]
    dot_general x34 -> x0, matrix products: 244 us -> none  [the longest x16 81.6 us: local(): jnp.einsum('hqd,hkd->hqk', q[:, lo:hi], k[:, :hi], preferred_element_type...]
    all_to_all x1 -> x0, blocking collectives: 102 us -> none  [local(): o = lax.all_to_all(o, 'seq', 0, 1, tiled=True)]
    reduce_sum x17 -> x0, other arithmetic: 54.5 us -> none  [the longest x16 51.4 us: local(): pr = jax.nn.softmax(sc, axis=-1).astype(jnp.bfloat16)]
    unnamed x65 -> x0, local copies, waits for them, and re-layouts: 31.1 us -> none
    all_to_all x1 -> x0, starting transfers between devices: 22.3 us -> none  [local(): buf = lax.all_to_all(buf, 'seq', 2, 1, tiled=True)]
    all_to_all x1 -> x0, local copies, waits for them, and re-layouts: 16.5 us -> none  [local(): buf = lax.all_to_all(buf, 'seq', 2, 1, tiled=True)]
  transfers between devices with their start and end apart: 1 -> 0, of which waited for: 1 -> 0; matrix products, arithmetic and copies ran while one was open for 0% -> 0% of each run, Pallas kernels for 0% -> 0%
where the time goes in v2:
time: 340 us; the launch traced here: 338 us
  Pallas kernels  334 us (98%)
  other arithmetic  4.47 us (1%)
    pallas_call x1, Pallas kernels, _sublayer(): pl.pallas_call(functools.partial(_body, p), in_specs=[any_, vm, any_, any...  334 us

profile of v2, /device:TPU:21, one launch (start us, length us, event | category | flops | bytes accessed | tf_op | source)
XLA Modules:
  0.0 338.4 jit_solution(15592257988196594746)
XLA Ops:
  0.0 333.9 %sublayer.1 = (bf16[512,4096]{1,0:T(8,128)(2,1)}, bf16[24,4096,256]{2,1,0:T(8,128)(2,1)}, bf16[5,2,2,256,4096]{4,3,2,1,0:T(8,128)(2,1)}) custom-call(bf16[512,4096]{1,0:T(8,128)(2,1)} %x_ref.1, f32[1,4096]{1,0:T(1,128)} %bitcast.1, bf16[4096,3,16,256]{3,2,1,0:T(8,128)(2,1)} %w_ref.1, bf16[16,256,4096]{2,1,0:T(8,128)(2,1)} %wo_ref.1, ...), custom_call_target="tpu_custom_call" | custom-call | tf_op jit(solution)/shard_map/sublayer/pallas_call | solution.py:668
  333.9 4.5 %broadcast_add_fusion = bf16[512,4096]{1,0:T(8,128)(2,1)} fusion(bf16[512,4096]{1,0:T(8,128)(2,1)} %get-tuple-element.6, bf16[]{:T(256)S(6)} %convert_element_type.3), kind=kLoop, calls=%fused_computation | loop fusion | flops 2097152 | bytes 8388610 | tf_op jit(solution)/shard_map/add | solution.py:691

commit v3 on v2

--- a/solution.py
+++ b/solution.py
@@ -562,14 +562,15 @@
     nw = dm // 2
     cw = 2 * R
     ncol = nw // cw
-    groups = ((0, 1, 2, 3), (4, 5, 6, 7), (8, 9, 14, 15), (10, 12), (11, 13))
+    groups = ((0, 1, 2, 3), (4, 5, 6, 7), (8, 9, 14, 15), (10, 11, 12, 13))
+    early = ((6, 7, 14, 15), groups[0], (4, 5, 8, 9), groups[3])
 
     def piece(n, k):
-        return _pick(n, [gr[k] if k < len(gr) else gr[0] for gr in groups])
-
-    def wo_load(wv, n, half, ks):
+        return jnp.where(chip >= ng, _pick(n, [gr[k] for gr in groups]), _pick(n, [gr[k] for gr in early]))
+
+    def wo_load(wv, n, half):
         sl, out = _rem3(2 * n + half), []
-        for k in ks:
+        for k in range(4):
             i = piece(n, k)
             gg = lax.rem(grp + _pick(_half(_rem8(i)), (2, 1, ng - 1, 0)), ng)
             head = hc * jnp.where(_odd(i) == 0, core, 1 - core) + hl * gg + _div8(i)
@@ -579,12 +580,7 @@
     def wo_start(wv, n, half):
         @pl.when(n < len(groups))
         def _():
-            for cp in wo_load(wv, n, half, (0, 1)):
-                cp.start()
-
-        @pl.when(n < 3)
-        def _():
-            for cp in wo_load(wv, n, half, (2, 3)):
+            for cp in wo_load(wv, n, half):
                 cp.start()
 
     def finish(yb, wv):
@@ -603,43 +599,41 @@
                 return c
             _loop(ncol, fill)
 
-        def out(size, n, c):
+        def out(n, c):
             for half in TWO:
                 sl = _rem3(2 * n + half)
                 wo_start(wv, n + 1, half)
                 if half == 0:
-                    for k in range(size):
+                    for k in range(4):
                         i = piece(n, k)
 
                         @pl.when(_rem8(i) != 6)
                         def _(i=i):
                             o_send(i).wait()
-                for cp in wo_load(wv, n, half, range(size)):
+                for cp in wo_load(wv, n, half):
                     cp.wait()
-                oo = jnp.concatenate([og[piece(n, k)] for k in range(size)], axis=-1)
+                oo = jnp.concatenate([og[piece(n, k)] for k in range(4)], axis=-1)
 
                 def cols(i, c2, half=half, sl=sl, oo=oo):
                     at = pl.ds(pl.multiple_of(i * cw, cw), cw)
-                    ww = jnp.concatenate([wv[sl, k, :, at] for k in range(size)], axis=0)
+                    ww = jnp.concatenate([wv[sl, k, :, at] for k in range(4)], axis=0)
                     a = jnp.dot(oo, ww, preferred_element_type=F32)
                     tops[half][i] = tops[half][i] + a[:R]
                     acc[half * ncol + i] = acc[half * ncol + i] + a[R:]
                     return c2
                 _loop(ncol, cols)
 
-                if size == 2:
-                    @pl.when(n == len(groups) - 1)
-                    def _(half=half):
-                        def store(i, c2):
-                            to = pl.ds(pl.multiple_of(half * nw + i * cw, cw), cw)
-                            yb[:R, to] = tops[half][i].astype(BF)
-                            yb[R:, to] = acc[half * ncol + i].astype(BF)
-                            pltpu.make_async_copy(yb.at[:, to], y_ref.at[:, to], wt_sem.at[0]).start()
-                            return c2
-                        _loop(ncol, store)
+                @pl.when(n == len(groups) - 1)
+                def _(half=half):
+                    def store(i, c2):
+                        to = pl.ds(pl.multiple_of(half * nw + i * cw, cw), cw)
+                        yb[:R, to] = tops[half][i].astype(BF)
+                        yb[R:, to] = acc[half * ncol + i].astype(BF)
+                        pltpu.make_async_copy(yb.at[:, to], y_ref.at[:, to], wt_sem.at[0]).start()
+                        return c2
+                    _loop(ncol, store)
             return c
-        _loop(3, functools.partial(out, 4))
-        lax.fori_loop(3, len(groups), functools.partial(out, 2), 0)
+        _loop(len(groups), out)
         pltpu.make_async_copy(yb, y_ref, wt_sem.at[0]).wait()
 
     pl.run_scoped(finish, pltpu.VMEM((qb, dm), BF), pltpu.VMEM((3, 4, R, nw), BF))

time: 340 us -> 342 us (level)
  no operation moved by 1% of the time
where the time goes in v3:
time: 342 us; the launch traced here: 340 us
  Pallas kernels  336 us (98%)
  other arithmetic  4.47 us (1%)
    pallas_call x1, Pallas kernels, _sublayer(): pl.pallas_call(functools.partial(_body, p), in_specs=[any_, vm, any_, any...  336 us

profile of v3, /device:TPU:21, one launch (start us, length us, event | category | flops | bytes accessed | tf_op | source)
XLA Modules:
  0.0 340.3 jit_solution(3888878802729456717)
XLA Ops:
  0.0 335.9 %sublayer.1 = (bf16[512,4096]{1,0:T(8,128)(2,1)}, bf16[24,4096,256]{2,1,0:T(8,128)(2,1)}, bf16[5,2,2,256,4096]{4,3,2,1,0:T(8,128)(2,1)}) custom-call(bf16[512,4096]{1,0:T(8,128)(2,1)} %x_ref.1, f32[1,4096]{1,0:T(1,128)} %bitcast.1, bf16[4096,3,16,256]{3,2,1,0:T(8,128)(2,1)} %w_ref.1, bf16[16,256,4096]{2,1,0:T(8,128)(2,1)} %wo_ref.1, ...), custom_call_target="tpu_custom_call" | custom-call | tf_op jit(solution)/shard_map/sublayer/pallas_call | solution.py:662
  335.9 4.5 %broadcast_add_fusion = bf16[512,4096]{1,0:T(8,128)(2,1)} fusion(bf16[512,4096]{1,0:T(8,128)(2,1)} %get-tuple-element.6, bf16[]{:T(256)S(6)} %convert_element_type.3), kind=kLoop, calls=%fused_computation | loop fusion | flops 2097152 | bytes 8388610 | tf_op jit(solution)/shard_map/add | solution.py:685
